TPU v7x, 256 devices: a 8x8x2 block of a 8x8x16 slice. The times are simulated.
256 devices in a mesh: parts: 2 (over z), seq: 128 (over x, y, core).
Axes of the slice: x: 8, y: 8, z: 2, core: 2. Of those that a mesh axis runs over, the one named last changes fastest.
The devices are a block of a 8x8x16 slice.
Arguments:
- token_ids: int32 [4, 4], P(None, 'parts'), parts along dimension 1, may hold values from 0 to 76031
- lengths: int32 [4], P('parts'), parts along dimension 0, may hold values from 24576 to 32768, as said below
- embed_table: bfloat16 [76032, 5120], P('seq'), may hold values from -6 to 6
- attn_gain: bfloat16 [5120], replicated, may hold values from 0.25 to 1.75
- w_qkv: bfloat16 [5120, 7168], P('seq'), may hold values from -0.3125 to 0.3125
- qkv_bias: float32 [7168], replicated, may hold values from -8 to 8
- cache_keys: bfloat16 [4, 32768, 1024], P('parts', 'seq'), parts along dimension 0, may hold values from -300 to 300
- cache_values: bfloat16 [4, 32768, 1024], P('parts', 'seq'), parts along dimension 0, may hold values from -6 to 6
- w_out: bfloat16 [5120, 5120], P(None, 'seq'), may hold values from -0.078125 to 0.078125
- mlp_gain: bfloat16 [5120], replicated, may hold values from 0.25 to 1.75
- w_gate: bfloat16 [5120, 16384], P(None, 'seq'), may hold values from -0.078125 to 0.078125
- w_up: bfloat16 [5120, 16384], P(None, 'seq'), may hold values from -0.078125 to 0.078125
- w_down: bfloat16 [16384, 5120], P('seq'), may hold values from -0.1875 to 0.1875
Outputs:
- attended: bfloat16 [4, 4, 5120], P(None, 'parts'), parts along dimension 1
- layer_out: bfloat16 [4, 4, 5120], P(None, 'parts', 'seq'), parts along dimension 1
There are 2 independent parts, one for each index of `parts`. A program takes and returns all parts, laid end to end along the dimension named above; an argument that names none is the same for every part. Nothing has to cross between parts.
Inputs may be any that keep to these rules, and one draw needn't show every extreme that they name: Cache positions lengths[b] and later are unused; the first prompt fills the whole cache of 32768 positions.
All inputs are finite; a program needn't handle non-finite values.
Results may differ from a plain program's by a relative error of at most 0.017.
The roundings to bfloat16 on the way count: a program that leaves them out, or rounds other values in their place, can miss the bound.
Values may be sent and summed in bfloat16 or wider, within the bound.
No kernel may reach another device: no remote copies, remote signals or barrier semaphores. Data moves between devices by JAX's collectives and lax.ppermute only.
A program may use at most 128 MiB of HBM per device.

v0:
```python
import math
import jax
import jax.numpy as jnp
from jax import lax
from jax.sharding import Mesh
from jax.sharding import PartitionSpec as P

HEADS = 40
KV_HEADS = 8
HEAD_DIM = 128
SEQ = ("seq_0", "seq_1", "seq_2")
NORM_EPS = 1e-06
ROPE_BASE = 1000000.0
MASKED = -1e30


def gathered_once(array, axis):
    leaves = jax.tree.leaves(array)
    order = sorted(range(len(leaves)), key=lambda k: -leaves[k].size)
    width = (1, *leaves[order[0]].shape)[-1]
    lines = [
        jnp.pad(leaves[k].reshape(-1), (0, -leaves[k].size % width)).reshape(-1, width)
        for k in order
    ]
    both, at, found = (lax.all_gather(jnp.concatenate(lines), axis), 0, {})
    for k, line in zip(order, lines):
        slab = both[:, at : at + len(line)].reshape(len(both), -1)
        found[k] = slab[:, : leaves[k].size].reshape(-1, *leaves[k].shape)
        at += len(line)
    numbers = iter(range(len(leaves)))
    return jax.tree.map(lambda _: found[next(numbers)], array)


def combined_by_axis(array, axes, combine):
    for axis in axes:
        pieces = gathered_once(array, axis)
        array = jax.tree.map(lambda part: part[0], pieces)
        for k in range(1, lax.axis_size(axis)):
            array = combine(array, jax.tree.map(lambda part: part[k], pieces))
    return array


def sum_in_order(parts, axes, order):
    dims = [lax.axis_size(a) for a in axes]
    parts = parts.reshape(*dims, *parts.shape[1:])
    parts = parts.transpose(*order, *range(len(axes), parts.ndim))
    parts = parts.reshape(-1, *parts.shape[len(axes) :])
    for k in order:
        parts = lax.psum_scatter(parts, axes[k], scatter_dimension=0, tiled=True)
    return parts[0]


def cut_along(array, dim, devices):
    before, after = (array.shape[:dim], array.shape[dim + 1 :])
    return jnp.moveaxis(array.reshape(*before, devices, -1, *after), dim, 0)


def scatter_axes(array, axes, order, dim):
    devices = lax.axis_size(axes)
    return sum_in_order(cut_along(array, dim, devices), axes, order)


def rms_normalize(rows, gain):
    mean_square = jnp.mean(rows * rows, axis=-1, keepdims=True)
    return (rows * lax.rsqrt(mean_square + NORM_EPS) * gain.astype(jnp.float32)).astype(
        jnp.bfloat16
    )


def rotate(vectors, positions):
    half_dim = vectors.shape[-1] // 2
    frequency = ROPE_BASE ** (-2.0 * jnp.arange(half_dim, dtype=jnp.float32) / vectors.shape[-1])
    angles = positions.astype(jnp.float32)[..., None, None] * frequency
    cosine = jnp.cos(angles)
    sine_part = jnp.sin(angles)
    widened = vectors.astype(jnp.float32)
    first_half = widened[..., :half_dim]
    second = widened[..., half_dim:]
    joined = jnp.concatenate(
        [first_half * cosine - second * sine_part, second * cosine + first_half * sine_part],
        axis=-1,
    )
    return joined.astype(jnp.bfloat16)


def combine_partials(earlier, latter):
    top_one, total_one, sum_one = earlier
    top_two, total_two, sum_two = latter
    joined_top = jnp.maximum(top_one, top_two)
    scale_one = jnp.exp(top_one - joined_top)
    scale_two = jnp.exp(top_two - joined_top)
    return (
        joined_top,
        total_one * scale_one + total_two * scale_two,
        sum_one * scale_one[..., None] + sum_two * scale_two[..., None],
    )


def body(
    token_ids,
    lengths,
    embed_table,
    attn_gain,
    w_qkv,
    qkv_bias,
    cache_keys,
    cache_values,
    w_out,
    mlp_gain,
    w_gate,
    w_up,
    w_down,
):
    rank = lax.axis_index(SEQ)
    step_count, batch_count = token_ids.shape
    model_width = embed_table.shape[1]
    vocab_rows = embed_table.shape[0]
    query_width = HEADS * HEAD_DIM
    key_width = KV_HEADS * HEAD_DIM
    group_size = HEADS // KV_HEADS
    local_ids = token_ids - rank * vocab_rows
    inside = (local_ids >= 0) & (local_ids < vocab_rows)
    picked = jnp.take(embed_table, jnp.clip(local_ids, 0, vocab_rows - 1), axis=0)
    partial_rows = jnp.where(inside[..., None], picked.astype(jnp.float32), 0.0)
    stream = lax.psum(partial_rows, SEQ)
    normed = rms_normalize(stream, attn_gain).reshape(-1, model_width)
    feature_rows = w_qkv.shape[0]
    normed_local = lax.dynamic_slice_in_dim(normed, rank * feature_rows, feature_rows, 1)
    joint_partial = jnp.dot(normed_local, w_qkv, preferred_element_type=jnp.float32)
    joint_summed = lax.psum(joint_partial, SEQ)
    joint = (joint_summed + qkv_bias).astype(jnp.bfloat16).reshape(step_count, batch_count, -1)
    query_part = joint[..., :query_width].reshape(step_count, batch_count, HEADS, HEAD_DIM)
    key_part = joint[..., query_width : query_width + key_width].reshape(
        step_count, batch_count, KV_HEADS, HEAD_DIM
    )
    value_part = joint[..., query_width + key_width :].reshape(
        step_count, batch_count, KV_HEADS, HEAD_DIM
    )
    positions = lengths[None, :] + jnp.arange(step_count, dtype=jnp.int32)[:, None]
    queries = rotate(query_part, positions)
    new_keys = rotate(key_part, positions)
    grouped = queries.reshape(step_count, batch_count, KV_HEADS, group_size, HEAD_DIM)
    score_scale = 1.0 / math.sqrt(HEAD_DIM)
    local_len = cache_keys.shape[1]
    key_blocks = cache_keys.reshape(batch_count, local_len, KV_HEADS, HEAD_DIM)
    value_blocks = cache_values.reshape(batch_count, local_len, KV_HEADS, HEAD_DIM)
    scores = (
        jnp.einsum("sbkgd,bpkd->bkgsp", grouped, key_blocks, preferred_element_type=jnp.float32)
        * score_scale
    )
    places = rank * local_len + jnp.arange(local_len, dtype=jnp.int32)
    valid = (places[None, :] < lengths[:, None])[:, None, None, None, :]
    masked = jnp.where(valid, scores, MASKED)
    local_top = jnp.max(masked, axis=-1)
    weights = jnp.where(valid, jnp.exp(masked - local_top[..., None]), 0.0)
    local_total = jnp.sum(weights, axis=-1)
    local_sum = jnp.einsum(
        "bkgsp,bpkd->bkgsd",
        weights.astype(jnp.bfloat16),
        value_blocks,
        preferred_element_type=jnp.float32,
    )
    merged_top, merged_total, merged_sum = combined_by_axis(
        (local_top, local_total, local_sum), SEQ, combine_partials
    )
    new_scores = (
        jnp.einsum("sbkgd,tbkd->bkgst", grouped, new_keys, preferred_element_type=jnp.float32)
        * score_scale
    )
    step_index = jnp.arange(step_count, dtype=jnp.int32)
    causal = step_index[:, None] >= step_index[None, :]
    new_masked = jnp.where(causal, new_scores, MASKED)
    final_top = jnp.maximum(merged_top, jnp.max(new_masked, axis=-1))
    rescale = jnp.exp(merged_top - final_top)
    new_weights = jnp.where(causal, jnp.exp(new_masked - final_top[..., None]), 0.0)
    final_total = merged_total * rescale + jnp.sum(new_weights, axis=-1)
    final_sum = merged_sum * rescale[..., None] + jnp.einsum(
        "bkgst,tbkd->bkgsd",
        new_weights.astype(jnp.bfloat16),
        value_part,
        preferred_element_type=jnp.float32,
    )
    attended = jnp.transpose(final_sum / final_total[..., None], (3, 0, 1, 2, 4))
    attended = attended.reshape(step_count, batch_count, query_width).astype(jnp.bfloat16)
    shard_cols = w_out.shape[1]
    projected = jnp.dot(
        attended.reshape(-1, query_width), w_out, preferred_element_type=jnp.float32
    )
    stream_shard = lax.dynamic_slice_in_dim(stream, rank * shard_cols, shard_cols, 2)
    mid_shard = stream_shard + projected.reshape(step_count, batch_count, shard_cols)
    mid_rows = lax.all_gather(mid_shard, SEQ, axis=2, tiled=True)
    normed_mid = rms_normalize(mid_rows, mlp_gain)
    flat_rows = normed_mid.reshape(-1, model_width)
    gate = jnp.dot(flat_rows, w_gate, preferred_element_type=jnp.float32)
    upper = jnp.dot(flat_rows, w_up, preferred_element_type=jnp.float32)
    hidden = (jax.nn.silu(gate) * upper).astype(jnp.bfloat16)
    down_terms = jnp.dot(hidden, w_down, preferred_element_type=jnp.float32).reshape(
        step_count, batch_count, model_width
    )
    summed = scatter_axes(down_terms, SEQ, (2, 1, 0), 2)
    layer_out = (mid_shard + summed).astype(jnp.bfloat16)
    return (attended, layer_out)


def solution(mesh):
    finer = Mesh(
        mesh.devices.reshape(mesh.shape["parts"], 8, 8, 2), ("parts", "seq_0", "seq_1", "seq_2")
    )
    return jax.shard_map(
        body,
        mesh=finer,
        in_specs=(
            P(None, "parts"),
            P("parts"),
            P(SEQ, None),
            P(),
            P(SEQ, None),
            P(),
            P("parts", SEQ, None),
            P("parts", SEQ, None),
            P(None, SEQ),
            P(),
            P(None, SEQ),
            P(None, SEQ),
            P(SEQ, None),
        ),
        out_specs=(P(None, "parts", None), P(None, "parts", SEQ)),
        check_vma=False,
    )
```

profile of v0, /device:TPU:528, one launch (start us, length us, event | category | flops | bytes accessed | tf_op | source)
XLA Modules:
  0.0 717.2 jit_solution(17745230185070453889)
XLA Ops:
  8.3 4.2 gather_fusion
  14.4 1.1 copy-done.3
  15.8 1.1 bitcast_bitcast_fusion
  16.9 195.6 %all-reduce.14.cloned.1.call-done = f32[4,2,5120]{2,1,0:T(2,128)} async-done(((f32[4,2,5120]{2,1,0:T(2,128)}), f32[4,2,5120]{2,1,0:T(2,128)}) %all-reduce.14.cloned.1.call-update) | async-done | bytes 163856 | tf_op jit(solution)/shard_map/psum | solution.py:125
  212.4 1.1 multiply_reduce_fusion.1
  213.5 1.1 multiply_convert_fusion.1
  214.6 1.0 fusion.77
  215.8 181.4 %all-reduce.16.cloned.1.call-done = f32[8,7168]{1,0:T(8,128)} async-done(((f32[8,7168]{1,0:T(8,128)}), f32[8,7168]{1,0:T(8,128)}) %all-reduce.16.cloned.1.call-update) | async-done | bytes 229392 | tf_op jit(solution)/shard_map/psum | solution.py:130
  397.2 1.0 add_convert_fusion
  400.1 1.5 fusion.9
  402.4 38.6 %all-gather.9.cloned.1.call-done = f32[8,326,128]{2,1,0:T(8,128)} async-done(((f32[1,326,128]{2,1,0:T(8,128)}), f32[8,326,128]{2,1,0:T(8,128)}) %all-gather.9.cloned.1.call-update) | async-done | bytes 1335312 | tf_op jit(solution)/shard_map/all_gather | solution.py:25
  442.1 2.0 fusion.39
  446.0 38.5 %all-gather.11.cloned.1.call-done = f32[8,326,128]{2,1,0:T(8,128)} async-done(((f32[1,326,128]{2,1,0:T(8,128)}), f32[8,326,128]{2,1,0:T(8,128)}) %all-gather.11.cloned.1.call-update) | async-done | bytes 1335312 | tf_op jit(solution)/shard_map/all_gather | solution.py:25
  485.6 2.0 fusion.18
  487.6 2.1 all-gather.5
  493.9 56.9 %all_gather.27 = f32[4,2,5120]{0,1,2:T(2,128)} all-gather(f32[4,2,40]{0,1,2:T(2,128)S(1)} %copy.230), channel_id=1, replica_groups=mesh['parts'=2,'seq_0'=8,'seq_1'=8,'seq_2'=2] {'seq_0','seq_1','seq_2'}, dimensions={2}, use_global_device_ids=true | all-gather | bytes 165120 | tf_op jit(solution)/shard_map/all_gather | solution.py:191
  550.8 5.6 copy.233
  556.5 7.0 multiply_reduce_fusion
  564.2 1.9 fusion.8
  566.7 1.1 copy.236
  569.3 30.1 %all-reduce.18.cloned.1.call-done = f32[128,4,2,40]{3,1,2,0:T(4,128)} async-done(((f32[128,4,2,40]{3,1,2,0:T(4,128)}), f32[128,4,2,40]{3,1,2,0:T(4,128)}) %all-reduce.18.cloned.1.call-update) | async-done | bytes 163856
  599.4 1.7 constant_dynamic-slice_fusion.2
  603.0 75.6 %all-reduce.20.cloned.1.call-done = f32[64,4,2,40]{3,1,2,0:T(4,128)} async-done(((f32[64,4,2,40]{3,1,2,0:T(4,128)}), f32[64,4,2,40]{3,1,2,0:T(4,128)}) %all-reduce.20.cloned.1.call-update) | async-done | bytes 81936
  679.4 29.7 %all-reduce.8 = f32[8,4,2,40]{3,1,2,0:T(4,128)S(1)} all-reduce(f32[8,4,2,40]{3,1,2,0:T(4,128)S(1)} %constant_dynamic-slice_fusion.1), channel_id=7, replica_groups=mesh['parts'=2,'seq_0'=8,'seq_1'=8,'seq_2'=2] {'seq_0'}, use_global_device_ids=true, to_apply=%region_10.11.clone | all-reduce | flops 2560 | bytes 20480
  (145 shorter events, 19.3 us)
Async XLA Ops:
  7.2 557.1 %copy-start = (bf16[128,5120]{1,0:T(8,128)(2,1)S(1)}, bf16[128,5120]{1,0:T(8,128)(2,1)}, u32[]{:S(2)}) copy-start(bf16[128,5120]{1,0:T(8,128)(2,1)} %param.25) | copy-start | bytes 3932164
  7.2 6.6 copy-start.7
  7.2 6.6 copy-start.9
  7.2 6.8 copy-start.2
  7.2 205.2 %all-reduce.14.cloned.1.call-start = ((), (), s32[]{:S(2)}) async-start(), calls=%async_computation | async-start | bytes 327680 | tf_op jit(solution)/shard_map/psum | solution.py:125
  13.7 383.5 %all-reduce.16.cloned.1.call-start = ((), (), s32[]{:S(2)}) async-start(), calls=%async_computation.1 | async-start | bytes 458752 | tf_op jit(solution)/shard_map/psum | solution.py:130
  14.3 1.2 copy-start.3
  15.8 198.8 %copy-start.4 = (bf16[40,7168]{1,0:T(8,128)(2,1)S(1)}, bf16[40,7168]{1,0:T(8,128)(2,1)}, u32[]{:S(2)}) copy-start(bf16[40,7168]{1,0:T(8,128)(2,1)} %param.17) | copy-start | bytes 1720324
  16.9 380.3 %copy-start.6 = (f32[7168]{0:T(1024)S(1)}, f32[7168]{0:T(1024)}, u32[]{:S(2)}) copy-start(f32[7168]{0:T(1024)} %param.18) | copy-start | bytes 86020
  215.7 225.3 %all-gather.9.cloned.1.call-start = ((), (), s32[]{:S(2)}) async-start(), calls=%async_computation.2 | async-start | bytes 1511424 | tf_op jit(solution)/shard_map/all_gather | solution.py:25
  402.3 42.6 %copy-start.8 = (bf16[5120]{0:T(1024)(128)(2,1)S(1)}, bf16[5120]{0:T(1024)(128)(2,1)}, u32[]{:S(2)}) copy-start(bf16[5120]{0:T(1024)(128)(2,1)} %param.22) | copy-start | bytes 30724
  402.3 82.2 %all-gather.11.cloned.1.call-start = ((), (), s32[]{:S(2)}) async-start(), calls=%async_computation.3 | async-start | bytes 1511424 | tf_op jit(solution)/shard_map/all_gather | solution.py:25
  444.8 154.6 %all-reduce.18.cloned.1.call-start = ((), (), s32[]{:S(2)}) async-start(), calls=%async_computation.4 | async-start | bytes 1048576
  491.8 1.0 copy-start.10
  492.8 58.0 %copy-start.5 = (bf16[4,2,5120]{2,1,0:T(2,128)(2,1)}, bf16[4,2,5120]{2,1,0:T(2,128)(2,1)S(1)}, u32[]{:S(2)}) copy-start(bf16[4,2,5120]{2,1,0:T(2,128)(2,1)S(1)} %convert_element_type.84) | copy-start | bytes 245764
  556.5 7.5 %copy-start.1 = (bf16[5120,128]{1,0:T(8,128)(2,1)S(1)}, bf16[5120,128]{1,0:T(8,128)(2,1)}, u32[]{:S(2)}) copy-start(bf16[5120,128]{1,0:T(8,128)(2,1)} %param.23) | copy-start | bytes 3932164
  566.5 1.5 copy-start.13
  566.7 34.4 %copy-start.12 = (u32[256]{0:T(256)S(1)}, u32[256]{0:T(256)}, u32[]{:S(2)}) copy-start(u32[256]{0:T(256)} %constant.90) | copy-start | bytes 3076
  566.7 35.0 %copy-start.11 = (u32[256]{0:T(256)S(1)}, u32[256]{0:T(256)}, u32[]{:S(2)}) copy-start(u32[256]{0:T(256)} %constant.94) | copy-start | bytes 3076
  567.9 110.7 %all-reduce.20.cloned.1.call-start = ((), (), s32[]{:S(2)}) async-start(), calls=%async_computation.5 | async-start | bytes 524288
Sparse Core Ops, SparseCore 0:
  13.8 198.6 all-reduce.13
  215.8 181.3 all-reduce.15
  402.5 38.5 all-gather.8
  444.9 39.5 all-gather.10
  568.1 31.3 all-reduce.17
  601.6 77.0 all-reduce.19
where the time goes:
time: 718 us; the launch traced here: 717 us
  waiting for transfers between devices  560 us (78%)
  blocking collectives  88.7 us (12%)
  local copies, waits for them, and re-layouts  25.4 us (4%)
  other arithmetic  19.2 us (3%)
  between operations  16 us (2%)
  matrix products  7.37 us (1%)
    psum x1, waiting for transfers between devices, body(): stream = lax.psum(partial_rows, SEQ)  196 us
    psum x1, waiting for transfers between devices, body(): joint_summed = lax.psum(joint_partial, SEQ)  181 us
    unnamed x8, waiting for transfers between devices  106 us
    all_gather x2, waiting for transfers between devices, gathered_once(): both, at, found = (lax.all_gather(jnp.concatenate(lines), axis), 0, {})  77.1 us
    all_gather x1, blocking collectives, body(): mid_rows = lax.all_gather(mid_shard, SEQ, axis=2, tiled=True)  56.9 us
    unnamed x1, blocking collectives  29.7 us
  transfers between devices with their start and end apart: 6, of which 6 were waited for; matrix products, arithmetic and copies ran while one was open for 1% of the time, Pallas kernels for 0%

commit v1 on v0

--- a/solution.py
+++ b/solution.py
@@ -122,7 +122,7 @@
     inside = (local_ids >= 0) & (local_ids < vocab_rows)
     picked = jnp.take(embed_table, jnp.clip(local_ids, 0, vocab_rows - 1), axis=0)
     partial_rows = jnp.where(inside[..., None], picked.astype(jnp.float32), 0.0)
-    stream = lax.psum(partial_rows, SEQ)
+    stream = jnp.sum(lax.all_gather(partial_rows, SEQ), axis=0)
     normed = rms_normalize(stream, attn_gain).reshape(-1, model_width)
     feature_rows = w_qkv.shape[0]
     normed_local = lax.dynamic_slice_in_dim(normed, rank * feature_rows, feature_rows, 1)

time: 718 us -> 648 us (0.903)
  waiting for transfers between devices: 560 us -> 484 us
    psum x1 -> x0, waiting for transfers between devices: 196 us -> none  [body(): stream = lax.psum(partial_rows, SEQ)]
    all_gather x0 -> x1, waiting for transfers between devices: none -> 117 us  [body(): stream = jnp.sum(lax.all_gather(partial_rows, SEQ), axis=0)]
    reduce_sum x0 -> x1, other arithmetic: none -> 10.9 us  [body(): stream = jnp.sum(lax.all_gather(partial_rows, SEQ), axis=0)]
    reduce_sum x2, other arithmetic: 8.13 us -> 0.28 us  [rms_normalize(): mean_square = jnp.mean(rows * rows, axis=-1, keepdims=True)]
where the time goes in v1:
time: 648 us; the launch traced here: 647 us
  waiting for transfers between devices  484 us (75%)
  blocking collectives  88.7 us (14%)
  local copies, waits for them, and re-layouts  28.5 us (4%)
  other arithmetic  21.2 us (3%)
  between operations  16 us (2%)
  matrix products  7.73 us (1%)
    psum x1, waiting for transfers between devices, body(): joint_summed = lax.psum(joint_partial, SEQ)  184 us
    all_gather x1, waiting for transfers between devices, body(): stream = jnp.sum(lax.all_gather(partial_rows, SEQ), axis=0)  117 us
    unnamed x8, waiting for transfers between devices  106 us
    all_gather x2, waiting for transfers between devices, gathered_once(): both, at, found = (lax.all_gather(jnp.concatenate(lines), axis), 0, {})  77.1 us
    all_gather x1, blocking collectives, body(): mid_rows = lax.all_gather(mid_shard, SEQ, axis=2, tiled=True)  56.9 us
    unnamed x1, blocking collectives  29.7 us
  transfers between devices with their start and end apart: 6, of which 6 were waited for; matrix products, arithmetic and copies ran while one was open for 1% of the time, Pallas kernels for 0%

profile of v1, /device:TPU:528, one launch (start us, length us, event | category | flops | bytes accessed | tf_op | source)
XLA Modules:
  0.0 646.9 jit_solution(978731221250273729)
XLA Ops:
  8.3 4.2 gather_fusion
  13.7 1.3 copy.196
  15.0 1.5 copy.197
  17.2 1.3 bitcast_bitcast_fusion.1
  18.5 1.0 bitcast_bitcast_fusion
  19.6 117.1 %all-gather.10.cloned.1.call-done = f32[128,4,2,5120]{3,1,2,0:T(4,128)} async-done(((f32[1,4,2,5120]{3,1,2,0:T(4,128)}), f32[128,4,2,5120]{3,1,2,0:T(4,128)}) %all-gather.10.cloned.1.call-update) | async-done | bytes 20971536 | tf_op jit(solution)/shard_map/all_gather | solution.py:125
  136.7 10.9 %reduce_sum.47 = f32[4,2,5120]{2,0,1:T(4,128)S(1)} reduce(f32[128,4,2,5120]{3,1,2,0:T(4,128)} %all-gather.10.cloned.1.call-done, f32[]{:T(128)} %constant.18.clone.1), dimensions={0}, to_apply=%region_0.1 | reduce | flops 5201920 | bytes 21135364 | tf_op jit(solution)/shard_map/reduce_sum | solution.py:125
  148.2 2.0 fusion.78
  150.4 184.2 %all-reduce.13.cloned.1.call-done = f32[8,7168]{1,0:T(8,128)} async-done(((f32[8,7168]{1,0:T(8,128)}), f32[8,7168]{1,0:T(8,128)}) %all-reduce.13.cloned.1.call-update) | async-done | bytes 229392 | tf_op jit(solution)/shard_map/psum | solution.py:130
  334.6 1.0 add_convert_fusion
  337.5 1.5 fusion.9
  339.8 38.6 %all-gather.12.cloned.1.call-done = f32[8,326,128]{2,1,0:T(8,128)} async-done(((f32[1,326,128]{2,1,0:T(8,128)}), f32[8,326,128]{2,1,0:T(8,128)}) %all-gather.12.cloned.1.call-update) | async-done | bytes 1335312 | tf_op jit(solution)/shard_map/all_gather | solution.py:25
  379.5 2.0 fusion.39
  383.5 38.5 %all-gather.14.cloned.1.call-done = f32[8,326,128]{2,1,0:T(8,128)} async-done(((f32[1,326,128]{2,1,0:T(8,128)}), f32[8,326,128]{2,1,0:T(8,128)}) %all-gather.14.cloned.1.call-update) | async-done | bytes 1335312 | tf_op jit(solution)/shard_map/all_gather | solution.py:25
  423.0 2.0 fusion.18
  425.0 2.1 all-gather.5
  430.6 56.9 %all_gather.32 = f32[4,2,5120]{0,1,2:T(2,128)} all-gather(f32[4,2,40]{0,1,2:T(2,128)S(1)} %copy.169), channel_id=1, replica_groups=mesh['parts'=2,'seq_0'=8,'seq_1'=8,'seq_2'=2] {'seq_0','seq_1','seq_2'}, dimensions={2}, use_global_device_ids=true | all-gather | bytes 165120 | tf_op jit(solution)/shard_map/all_gather | solution.py:191
  487.5 5.8 copy.172
  494.0 1.9 fusion.8
  496.5 1.1 copy.175
  499.0 30.1 %all-reduce.15.cloned.1.call-done = f32[128,4,2,40]{3,1,2,0:T(4,128)} async-done(((f32[128,4,2,40]{3,1,2,0:T(4,128)}), f32[128,4,2,40]{3,1,2,0:T(4,128)}) %all-reduce.15.cloned.1.call-update) | async-done | bytes 163856
  529.1 1.7 constant_dynamic-slice_fusion.2
  532.8 75.6 %all-reduce.17.cloned.1.call-done = f32[64,4,2,40]{3,1,2,0:T(4,128)} async-done(((f32[64,4,2,40]{3,1,2,0:T(4,128)}), f32[64,4,2,40]{3,1,2,0:T(4,128)}) %all-reduce.17.cloned.1.call-update) | async-done | bytes 81936
  609.2 29.7 %all-reduce.8 = f32[8,4,2,40]{3,1,2,0:T(4,128)S(1)} all-reduce(f32[8,4,2,40]{3,1,2,0:T(4,128)S(1)} %constant_dynamic-slice_fusion.1), channel_id=7, replica_groups=mesh['parts'=2,'seq_0'=8,'seq_1'=8,'seq_2'=2] {'seq_0'}, use_global_device_ids=true, to_apply=%region_10.11.clone | all-reduce | flops 2560 | bytes 20480
  (138 shorter events, 19.0 us)
Async XLA Ops:
  7.2 486.8 %copy-start = (bf16[128,5120]{1,0:T(8,128)(2,1)S(1)}, bf16[128,5120]{1,0:T(8,128)(2,1)}, u32[]{:S(2)}) copy-start(bf16[128,5120]{1,0:T(8,128)(2,1)} %param.25) | copy-start | bytes 3932164
  7.2 6.3 copy-start.6
  7.2 6.5 %copy-start.2 = (bf16[2,256,1024]{2,1,0:T(8,128)(2,1)S(1)}, bf16[2,256,1024]{2,1,0:T(8,128)(2,1)}, u32[]{:S(2)}) copy-start(bf16[2,256,1024]{2,1,0:T(8,128)(2,1)} %param.19) | copy-start | bytes 3145732
  7.2 129.4 %all-gather.10.cloned.1.call-start = ((), (), s32[]{:S(2)}) async-start(), calls=%async_computation | async-start | bytes 21135360 | tf_op jit(solution)/shard_map/all_gather | solution.py:125
  13.4 321.2 %all-reduce.13.cloned.1.call-start = ((), (), s32[]{:S(2)}) async-start(), calls=%async_computation.1 | async-start | bytes 458752 | tf_op jit(solution)/shard_map/psum | solution.py:130
  147.6 187.0 %copy-start.4 = (f32[7168]{0:T(1024)S(1)}, f32[7168]{0:T(1024)}, u32[]{:S(2)}) copy-start(f32[7168]{0:T(1024)} %param.18) | copy-start | bytes 86020
  150.3 228.1 %all-gather.12.cloned.1.call-start = ((), (), s32[]{:S(2)}) async-start(), calls=%async_computation.2 | async-start | bytes 1511424 | tf_op jit(solution)/shard_map/all_gather | solution.py:25
  339.7 42.6 %copy-start.5 = (bf16[5120]{0:T(1024)(128)(2,1)S(1)}, bf16[5120]{0:T(1024)(128)(2,1)}, u32[]{:S(2)}) copy-start(bf16[5120]{0:T(1024)(128)(2,1)} %param.22) | copy-start | bytes 30724
  339.8 82.2 %all-gather.14.cloned.1.call-start = ((), (), s32[]{:S(2)}) async-start(), calls=%async_computation.3 | async-start | bytes 1511424 | tf_op jit(solution)/shard_map/all_gather | solution.py:25
  382.2 146.9 %all-reduce.15.cloned.1.call-start = ((), (), s32[]{:S(2)}) async-start(), calls=%async_computation.4 | async-start | bytes 1048576
  429.2 1.0 copy-start.7
  430.2 57.3 %copy-start.3 = (bf16[4,2,5120]{2,1,0:T(2,128)(2,1)}, bf16[4,2,5120]{2,1,0:T(2,128)(2,1)S(1)}, u32[]{:S(2)}) copy-start(bf16[4,2,5120]{2,1,0:T(2,128)(2,1)S(1)} %convert_element_type.92) | copy-start | bytes 245764
  487.5 6.1 copy-start.1
  496.3 1.5 copy-start.10
  496.4 34.4 %copy-start.9 = (u32[256]{0:T(256)S(1)}, u32[256]{0:T(256)}, u32[]{:S(2)}) copy-start(u32[256]{0:T(256)} %constant.90) | copy-start | bytes 3076
  496.4 35.0 %copy-start.8 = (u32[256]{0:T(256)S(1)}, u32[256]{0:T(256)}, u32[]{:S(2)}) copy-start(u32[256]{0:T(256)} %constant.94) | copy-start | bytes 3076
  497.7 110.7 %all-reduce.17.cloned.1.call-start = ((), (), s32[]{:S(2)}) async-start(), calls=%async_computation.5 | async-start | bytes 524288
Sparse Core Ops, SparseCore 0:
  13.5 123.0 all-gather.9
  150.4 184.1 all-reduce.12
  339.9 38.5 all-gather.11
  382.3 39.5 all-gather.13
  497.8 31.3 all-reduce.14
  531.3 77.0 all-reduce.16
